TPU v7x, 32 devices: a whole 2x2x4 slice. The times are simulated.
32 devices in a mesh: gx: 2 (over y), gy: 4 (over x, core), gz: 4 (over z).
Axes of the slice: x: 2, y: 2, z: 4, core: 2. Of those that a mesh axis runs over, the one named last changes fastest.
Arguments:
- head_out: bfloat16 [768, 4096], P(('gy', 'gx'), 'gz'), may hold values from -6 to 6
- out_weight: bfloat16 [4096, 4096], P('gz', ('gx', 'gy')), may hold values from -0.09375 to 0.09375
- residual: bfloat16 [768, 4096], P(('gy', 'gz'), 'gx'), may hold values from -84 to 84
- norm_gain: bfloat16 [4096], replicated, may hold values from 0.5 to 1.5
Outputs:
- hidden_out: bfloat16 [768, 4096], P(('gy', 'gz'), 'gx')
- normed: bfloat16 [768, 4096], P(('gy', 'gz'), 'gx')
All inputs are finite; a program needn't handle non-finite values.
Results may differ from a plain program's by a relative error of at most 0.0098.
Values may be sent and summed in bfloat16 or wider, within the bound.
A program may use at most 64 MiB of HBM per device.

v0:
```python
import jax
import jax.numpy as jnp
from jax import lax
from jax.sharding import PartitionSpec as P


def shards(head_out, out_weight, residual, norm_gain):
    weight_cols = lax.all_gather(out_weight, "gy", axis=1, tiled=True)
    gathered = lax.all_gather(head_out, "gx", axis=0, tiled=True)
    projected = lax.psum_scatter(
        jnp.dot(gathered, weight_cols, preferred_element_type=jnp.float32),
        "gz",
        scatter_dimension=0,
        tiled=True,
    )
    hidden = (residual.astype(jnp.float32) + projected).astype(jnp.bfloat16)
    gain_all = norm_gain.astype(jnp.float32)
    col_width = hidden.shape[1]
    groups = lax.axis_size("gx")
    widened = lax.optimization_barrier(hidden).astype(jnp.float32)
    squares = lax.psum(jnp.sum(widened * widened, axis=1), "gx")
    inverse = lax.rsqrt(squares / (col_width * groups) + 1e-05)
    gain_slice = lax.dynamic_slice_in_dim(gain_all, lax.axis_index("gx") * col_width, col_width, 0)
    normed = (widened * inverse[:, None] * gain_slice[None, :]).astype(jnp.bfloat16)
    return (hidden, normed)


def solution(mesh):
    in_specs = (P(("gy", "gx"), "gz"), P("gz", ("gx", "gy")), P(("gy", "gz"), "gx"), P())
    out_specs = (P(("gy", "gz"), "gx"), P(("gy", "gz"), "gx"))
    return jax.shard_map(shards, mesh=mesh, in_specs=in_specs, out_specs=out_specs, check_vma=False)
```

profile of v0, /device:TPU:0, one launch (start us, length us, event | category | flops | bytes accessed | tf_op | source)
XLA Modules:
  0.0 100.5 jit_solution(9989452801680639679)
XLA Ops:
  7.2 0.0 all-gather.2.cloned.1.call-start
  7.2 0.7 all-gather.2.cloned.1.call-update
  7.9 0.0 copy-start.2
  7.9 0.0 copy-start.1
  7.9 0.0 reduce-scatter.2.cloned.1.call-start
  8.0 9.0 %all_gather.6 = bf16[192,1024]{1,0:T(8,128)(2,1)S(1)} all-gather(bf16[96,1024]{1,0:T(8,128)(2,1)} %param.4), channel_id=1, replica_groups=mesh['gx'=2,'gy'=4,'gz'=4] {'gx'}, dimensions={0}, use_global_device_ids=true | all-gather | bytes 589824 | tf_op jit(solution)/shard_map/all_gather | solution.py:9
  16.9 29.8 %all-gather.2.cloned.1.call-done = bf16[1024,2048]{1,0:T(8,128)(2,1)} async-done(((bf16[1024,512]{1,0:T(8,128)(2,1)}), bf16[1024,2048]{1,0:T(8,128)(2,1)}) %all-gather.2.cloned.1.call-update) | async-done | bytes 4194320 | tf_op jit(solution)/shard_map/all_gather | solution.py:8
  46.7 4.3 %fusion.3 = f32[192,2048]{1,0:T(8,128)} fusion(bf16[192,1024]{1,0:T(8,128)(2,1)S(1)} %all_gather.6, bf16[1024,2048]{1,0:T(8,128)(2,1)} %all-gather.2.cloned.1.call-done), kind=kOutput, calls=%fused_computation.8 | convolution fusion | flops 805306368 | bytes 6160384 | tf_op jit(solution)/shard_map/dot_general | solution.py:11
  51.1 0.0 reduce-scatter.2.cloned.1.call-update
  51.1 0.0 copy-done.2
  51.1 35.6 %reduce-scatter.2.cloned.1.call-done = f32[48,2048]{1,0:T(8,128)} async-done(((f32[192,2048]{1,0:T(8,128)}), f32[48,2048]{1,0:T(8,128)}) %reduce-scatter.2.cloned.1.call-update) | async-done | bytes 393232 | tf_op jit(solution)/shard_map/reduce_scatter | solution.py:10
  86.7 0.0 copy-done.1
  86.7 1.0 %add_convert_fusion = bf16[48,2048]{1,0:T(8,128)(2,1)S(1)} fusion(f32[48,2048]{1,0:T(8,128)} %reduce-scatter.2.cloned.1.call-done, bf16[48,2048]{1,0:T(8,128)(2,1)S(1)} %copy-done.1), kind=kLoop, calls=%fused_computation.5 | loop fusion | flops 294912 | bytes 786432 | tf_op jit(solution)/shard_map/convert_element_type | solution.py:16
  87.7 0.0 copy-start
  87.8 0.1 fusion
  87.9 4.9 %psum.7 = f32[48]{0:T(128)S(1)} all-reduce(f32[48]{0:T(128)S(1)} %fusion), channel_id=1, replica_groups=mesh['gx'=2,'gy'=4,'gz'=4] {'gx'}, use_global_device_ids=true, to_apply=%region_2.0 | all-reduce | flops 48 | bytes 384 | tf_op jit(solution)/shard_map/psum | solution.py:21
  92.8 0.8 fusion.2
  93.6 0.0 copy-done
  (2 shorter events, 0.0 us)
Async XLA Ops:
  7.2 39.6 %all-gather.2.cloned.1.call-start = ((), (), s32[]{:S(2)}) async-start(), calls=%async_computation.1 | async-start | bytes 5242880 | tf_op jit(solution)/shard_map/all_gather | solution.py:8
  7.9 43.2 %copy-start.2 = (bf16[4096]{0:T(1024)(128)(2,1)S(1)}, bf16[4096]{0:T(1024)(128)(2,1)}, u32[]{:S(2)}) copy-start(bf16[4096]{0:T(1024)(128)(2,1)} %param.7) | copy-start | bytes 24580
  7.9 78.8 %copy-start.1 = (bf16[48,2048]{1,0:T(8,128)(2,1)S(1)}, bf16[48,2048]{1,0:T(8,128)(2,1)}, u32[]{:S(2)}) copy-start(bf16[48,2048]{1,0:T(8,128)(2,1)} %param.6) | copy-start | bytes 589828
  7.9 78.8 %reduce-scatter.2.cloned.1.call-start = ((), (), s32[]{:S(2)}) async-start(), calls=%async_computation.2 | async-start | bytes 1966080 | tf_op jit(solution)/shard_map/reduce_scatter | solution.py:10
  87.7 5.9 %copy-start = (bf16[48,2048]{1,0:T(8,128)(2,1)}, bf16[48,2048]{1,0:T(8,128)(2,1)S(1)}, u32[]{:S(2)}) copy-start(bf16[48,2048]{1,0:T(8,128)(2,1)S(1)} %add_convert_fusion) | copy-start | bytes 589828
Sparse Core Ops, SparseCore 0:
  9.5 37.1 all-gather.1
  51.2 35.4 reduce-scatter.1
where the time goes:
time: 101 us; the launch traced here: 100 us
  waiting for transfers between devices  66.1 us (65%)
  between operations  14.1 us (14%)
  blocking collectives  13.9 us (14%)
  matrix products  4.35 us (4%)
  other arithmetic  2 us (2%)
    reduce_scatter x1, waiting for transfers between devices, shards(): lax.psum_scatter(jnp.dot(gathered, weight_cols, preferred_element_type=jn...  35.6 us
    all_gather x1, waiting for transfers between devices, shards(): weight_cols = lax.all_gather(out_weight, 'gy', axis=1, tiled=True)  29.8 us
    all_gather x1, blocking collectives, shards(): gathered = lax.all_gather(head_out, 'gx', axis=0, tiled=True)  8.96 us
    psum x1, blocking collectives, shards(): squares = lax.psum(jnp.sum(widened * widened, axis=1), 'gx')  4.93 us
    dot_general x1, matrix products, shards(): jnp.dot(gathered, weight_cols, preferred_element_type=jnp.float32)  4.35 us
  transfers between devices with their start and end apart: 2, of which 2 were waited for; matrix products, arithmetic and copies ran while one was open for 0% of the time, Pallas kernels for 0%

commit v1 on v0

v1 whole, which is shorter than its diff:
```python
import functools

import jax
import jax.numpy as jnp
from jax import lax
from jax.experimental import pallas as pl
from jax.experimental.pallas import tpu as pltpu
from jax.sharding import PartitionSpec as P

MESH = pl.DeviceIdType.MESH
F32 = jnp.float32
BF16 = jnp.bfloat16
CORES = 2


def kernel(ny, ngy, nz, head_ref, w_ref, res_ref, gain_ref, hid_ref, nrm_ref,
           heads, w_own, w_other, res_v, send_buf, recv, own, sums,
           local_sem, w_send, w_recv, h_send, h_recv, p_send, p_recv, s_send, s_recv):
    nx = ngy // CORES
    y = lax.axis_index("gx")
    gy = lax.axis_index("gy")
    z = lax.axis_index("gz")
    x, core = lax.div(gy, CORES), lax.rem(gy, CORES)
    in_rows = head_ref.shape[0]
    out_rows, cols = res_ref.shape
    wc = w_ref.shape[1]
    per_block = nz // ny

    def at(dx, dy, dz):
        return (lax.rem(y + dy + ny, ny), lax.rem(x + dx + nx, nx) * CORES + core, lax.rem(z + dz + nz, nz))

    partner = (y, x * CORES + 1 - core, z)
    offsets = {(dx, dy, 0) for dx in range(nx) for dy in range(ny)} | {(dx, 0, dz) for dx in range(nx) for dz in range(nz)}
    offsets = sorted(offsets - {(0, 0, 0)})
    barrier = pltpu.get_barrier_semaphore()
    pl.semaphore_signal(barrier, inc=1, device_id=partner, device_id_type=MESH)
    for off in offsets:
        pl.semaphore_signal(barrier, inc=1, device_id=at(*off), device_id_type=MESH)

    head_in = pltpu.make_async_copy(head_ref, heads.at[0, 0], local_sem.at[0])
    w_in = pltpu.make_async_copy(w_ref, w_own, local_sem.at[1])
    res_in = pltpu.make_async_copy(res_ref, res_v, local_sem.at[2])
    head_in.start()
    w_in.start()
    res_in.start()
    head_in.wait()
    pl.semaphore_wait(barrier, len(offsets) + 1)

    blocks = sorted(((dx, dy) for dx in range(nx) for dy in range(ny)), key=lambda b: ((b[0] > 0) + (b[1] > 0), b))
    head_copies = {}
    for dx, dy in blocks[1:]:
        head_copies[dx, dy] = pltpu.make_async_remote_copy(
            src_ref=heads.at[0, 0], dst_ref=heads.at[dx, dy],
            send_sem=h_send.at[dx, dy], recv_sem=h_recv.at[dx, dy],
            device_id=at(-dx, -dy, 0), device_id_type=MESH)
        head_copies[dx, dy].start()
    w_in.wait()
    w_copy = pltpu.make_async_remote_copy(
        src_ref=w_own, dst_ref=w_other, send_sem=w_send, recv_sem=w_recv,
        device_id=partner, device_id_type=MESH)
    w_copy.start()

    def chunk(dx, dy, hr, j):
        to_z = lax.rem(y + dy, ny) * per_block + j
        dz = lax.rem(to_z - z + nz, nz)
        copy = pltpu.make_async_remote_copy(
            src_ref=send_buf.at[dx, dy, hr, pl.ds(j * out_rows, out_rows)],
            dst_ref=recv.at[dx, dz, hr],
            send_sem=p_send.at[dx, dy, hr, j], recv_sem=p_recv.at[dx, dz, hr],
            device_id=(y, lax.rem(x + dx, nx) * CORES + core, to_z), device_id_type=MESH)
        return to_z, copy

    for dx, dy in blocks:
        if (dx, dy) != (0, 0):
            head_copies[dx, dy].wait_recv()
        for hr in range(CORES):
            if (dx, dy) == (0, 0) and hr == 1:
                w_copy.wait_recv()
            part = jnp.dot(heads[dx, dy], (w_other if hr else w_own)[...], preferred_element_type=F32)
            send_buf[dx, dy, hr] = part.astype(BF16)
            for j in range(per_block):
                to_z, copy = chunk(dx, dy, hr, j)
                if dx:
                    copy.start()
                else:
                    pl.when(to_z != z)(copy.start)

                    @pl.when(to_z == z)
                    def _():
                        own[hr] = part[j * out_rows:(j + 1) * out_rows]

    res_in.wait()
    total = jnp.zeros((out_rows, 128), F32)
    for dx in range(nx):
        from_x = lax.rem(x - dx + nx, nx)
        for hr in range(CORES):
            half = core if hr == 0 else 1 - core
            where = pl.ds(pl.multiple_of((from_x * CORES + half) * wc, wc), wc)
            acc = own[hr] if dx == 0 else None
            for dz in range(nz):
                if (dx, dz) == (0, 0):
                    continue
                pltpu.make_async_remote_copy(
                    src_ref=send_buf.at[0, 0, hr, pl.ds(0, out_rows)], dst_ref=recv.at[dx, dz, hr],
                    send_sem=p_send.at[0, 0, hr, 0], recv_sem=p_recv.at[dx, dz, hr],
                    device_id=partner, device_id_type=MESH).wait_recv()
                term = recv[dx, dz, hr].astype(F32)
                acc = term if acc is None else acc + term
            hidden = (res_v[:, where].astype(F32) + acc).astype(BF16)
            hid_ref[:, where] = hidden
            wide = hidden.astype(F32)
            square = wide * wide
            for k in range(0, wc, 128):
                total = total + square[:, k:k + 128]
    sums[0] = jnp.broadcast_to(jnp.sum(total, axis=1, keepdims=True), (out_rows, 128))
    sum_copies = []
    for dy in range(1, ny):
        sum_copies.append(pltpu.make_async_remote_copy(
            src_ref=sums.at[0], dst_ref=sums.at[dy], send_sem=s_send.at[dy], recv_sem=s_recv.at[dy],
            device_id=at(0, -dy, 0), device_id_type=MESH))
        sum_copies[-1].start()

    w_copy.wait_send()
    for copy in head_copies.values():
        copy.wait_send()
    for dx, dy in blocks:
        for hr in range(CORES):
            for j in range(per_block):
                to_z, copy = chunk(dx, dy, hr, j)
                if dx:
                    copy.wait_send()
                else:
                    pl.when(to_z != z)(copy.wait_send)
    squares = sums[0]
    for dy, copy in enumerate(sum_copies, 1):
        copy.wait()
        squares = squares + sums[dy]
    inverse = lax.rsqrt(squares / (cols * ny) + 1e-05)[:, :1]
    gain = gain_ref[:, pl.ds(pl.multiple_of(y * cols, cols), cols)]
    nrm_ref[...] = (hid_ref[...].astype(F32) * inverse * gain).astype(BF16)


def shards(head_out, out_weight, residual, norm_gain):
    ny, ngy, nz = (lax.axis_size(a) for a in ("gx", "gy", "gz"))
    nx = ngy // CORES
    in_rows, depth = head_out.shape
    wc = out_weight.shape[1]
    out_rows, cols = residual.shape
    per_block = nz // ny
    any_spec = pl.BlockSpec(memory_space=pl.ANY)
    vmem = pl.BlockSpec(memory_space=pltpu.VMEM)
    dma = pltpu.SemaphoreType.DMA
    return pl.pallas_call(
        functools.partial(kernel, ny, ngy, nz),
        out_shape=[jax.ShapeDtypeStruct((out_rows, cols), BF16)] * 2,
        in_specs=[any_spec, any_spec, any_spec, vmem],
        out_specs=[vmem, vmem],
        scratch_shapes=[
            pltpu.VMEM((nx, ny, in_rows, depth), BF16),
            pltpu.VMEM((depth, wc), BF16),
            pltpu.VMEM((depth, wc), BF16),
            pltpu.VMEM((out_rows, cols), BF16),
            pltpu.VMEM((nx, ny, CORES, in_rows, wc), BF16),
            pltpu.VMEM((nx, nz, CORES, out_rows, wc), BF16),
            pltpu.VMEM((CORES, out_rows, wc), F32),
            pltpu.VMEM((ny, out_rows, 128), F32),
            dma((3,)), dma, dma, dma((nx, ny)), dma((nx, ny)),
            dma((nx, ny, CORES, per_block)), dma((nx, nz, CORES)),
            dma((ny,)), dma((ny,)),
        ],
        compiler_params=pltpu.CompilerParams(collective_id=0, has_side_effects=True),
    )(head_out, out_weight, residual, norm_gain.astype(F32).reshape(1, -1))


def solution(mesh):
    in_specs = (P(("gy", "gx"), "gz"), P("gz", ("gx", "gy")), P(("gy", "gz"), "gx"), P())
    out_specs = (P(("gy", "gz"), "gx"), P(("gy", "gz"), "gx"))
    return jax.shard_map(shards, mesh=mesh, in_specs=in_specs, out_specs=out_specs, check_vma=False)
```

time: 101 us -> 38.2 us (0.38)
  waiting for transfers between devices: 66.1 us -> 0 us
  Pallas kernels: 0 us -> 33.6 us
  blocking collectives: 13.9 us -> 0 us
  between operations: 14.1 us -> 0.65 us
  matrix products: 4.35 us -> 0 us
  local copies, waits for them, and re-layouts: 0.02 us -> 2.34 us
    reduce_scatter x1 -> x0, waiting for transfers between devices: 35.6 us -> none  [shards(): lax.psum_scatter(jnp.dot(gathered, weight_cols, preferred_element_type=jn...]
    pallas_call x0 -> x1, Pallas kernels: none -> 33.6 us  [shards(): pl.pallas_call(functools.partial(kernel, ny, ngy, nz), out_shape=[jax.Sha...]
    all_gather x1 -> x0, waiting for transfers between devices: 29.8 us -> none  [shards(): weight_cols = lax.all_gather(out_weight, 'gy', axis=1, tiled=True)]
    all_gather x1 -> x0, blocking collectives: 8.96 us -> none  [shards(): gathered = lax.all_gather(head_out, 'gx', axis=0, tiled=True)]
    psum x1 -> x0, blocking collectives: 4.93 us -> none  [shards(): squares = lax.psum(jnp.sum(widened * widened, axis=1), 'gx')]
    dot_general x1 -> x0, matrix products: 4.35 us -> none  [shards(): jnp.dot(gathered, weight_cols, preferred_element_type=jnp.float32)]
    unnamed x6 -> x4, local copies, waits for them, and re-layouts: 0.02 us -> 2.34 us
    convert_element_type x3 -> x0, other arithmetic: 1.84 us -> none  [the longest x1 1.03 us: shards(): hidden = (residual.astype(jnp.float32) + projected).astype(jnp.bfloat16)]
  transfers between devices with their start and end apart: 2 -> 0, of which waited for: 2 -> 0; matrix products, arithmetic and copies ran while one was open for 0% -> 0% of each run, Pallas kernels for 0% -> 0%
where the time goes in v1:
time: 38.2 us; the launch traced here: 37.9 us
  Pallas kernels  33.6 us (88%)
  local copies, waits for them, and re-layouts  2.34 us (6%)
  other arithmetic  1.3 us (3%)
  between operations  0.65 us (2%)
    pallas_call x1, Pallas kernels, shards(): pl.pallas_call(functools.partial(kernel, ny, ngy, nz), out_shape=[jax.Sha...  33.6 us
    unnamed x4, local copies, waits for them, and re-layouts  2.34 us
    reshape x1, other arithmetic, shards(): norm_gain.astype(F32).reshape(1, -1)  1.3 us

profile of v1, /device:TPU:0, one launch (start us, length us, event | category | flops | bytes accessed | tf_op | source)
XLA Modules:
  0.0 37.9 jit_solution(5450860740676771532)
XLA Ops:
  0.6 1.3 %reshape.11 = f32[4096]{0:T(1024)} convert(bf16[4096]{0:T(1024)(128)(2,1)} %param.7) | non-fusion elementwise | flops 4096 | bytes 24576 | tf_op jit(solution)/shard_map/reshape | solution.py:172
  1.9 33.6 %shard_map.59 = (bf16[48,2048]{1,0:T(8,128)(2,1)}, bf16[48,2048]{1,0:T(8,128)(2,1)}) custom-call(bf16[96,1024]{1,0:T(8,128)(2,1)} %head_ref.1, bf16[1024,512]{1,0:T(8,128)(2,1)} %w_ref.1, bf16[48,2048]{1,0:T(8,128)(2,1)} %res_ref.1, f32[1,4096]{1,0:T(1,128)} %bitcast.1), custom_call_target="tpu_custom_call" | custom-call | tf_op jit(solution)/shard_map/pallas_call | solution.py:153
  35.6 0.0 copy-start
  35.6 1.7 %copy.8 = bf16[48,2048]{1,0:T(8,128)(2,1)} copy(bf16[48,2048]{1,0:T(8,128)(2,1)} %get-tuple-element.4) | data formatting | bytes 393216
  37.2 0.0 copy-done
  37.2 0.7 %copy.9 = bf16[48,2048]{1,0:T(8,128)(2,1)} copy(bf16[48,2048]{1,0:T(8,128)(2,1)S(1)} %copy-done) | data formatting | bytes 393216
Async XLA Ops:
  35.6 1.7 %copy-start = (bf16[48,2048]{1,0:T(8,128)(2,1)S(1)}, bf16[48,2048]{1,0:T(8,128)(2,1)}, u32[]{:S(2)}) copy-start(bf16[48,2048]{1,0:T(8,128)(2,1)} %get-tuple-element.5) | copy-start | bytes 589828

commit v2 on v1

--- a/solution.py
+++ b/solution.py
@@ -14,8 +14,8 @@
 
 
 def kernel(ny, ngy, nz, head_ref, w_ref, res_ref, gain_ref, hid_ref, nrm_ref,
-           heads, w_own, w_other, res_v, send_buf, recv, own, sums,
-           local_sem, w_send, w_recv, h_send, h_recv, p_send, p_recv, s_send, s_recv):
+           heads, w_own, w_other, res_v, send_buf, recv, own, back, sums,
+           local_sem, w_send, w_recv, h_send, h_recv, p_send, p_recv, b_send, b_recv, s_send, s_recv):
     nx = ngy // CORES
     y = lax.axis_index("gx")
     gy = lax.axis_index("gy")
@@ -30,7 +30,7 @@
         return (lax.rem(y + dy + ny, ny), lax.rem(x + dx + nx, nx) * CORES + core, lax.rem(z + dz + nz, nz))
 
     partner = (y, x * CORES + 1 - core, z)
-    offsets = {(dx, dy, 0) for dx in range(nx) for dy in range(ny)} | {(dx, 0, dz) for dx in range(nx) for dz in range(nz)}
+    offsets = {(dx, dy, 0) for dx in range(nx) for dy in range(ny)} | {(0, 0, dz) for dz in range(nz)}
     offsets = sorted(offsets - {(0, 0, 0)})
     barrier = pltpu.get_barrier_semaphore()
     pl.semaphore_signal(barrier, inc=1, device_id=partner, device_id_type=MESH)
@@ -46,7 +46,7 @@
     head_in.wait()
     pl.semaphore_wait(barrier, len(offsets) + 1)
 
-    blocks = sorted(((dx, dy) for dx in range(nx) for dy in range(ny)), key=lambda b: ((b[0] > 0) + (b[1] > 0), b))
+    blocks = sorted(((dx, dy) for dx in range(nx) for dy in range(ny)), key=lambda b: ((b[0] > 0) + (b[1] > 0), -b[0], b))
     head_copies = {}
     for dx, dy in blocks[1:]:
         head_copies[dx, dy] = pltpu.make_async_remote_copy(
@@ -67,7 +67,7 @@
             src_ref=send_buf.at[dx, dy, hr, pl.ds(j * out_rows, out_rows)],
             dst_ref=recv.at[dx, dz, hr],
             send_sem=p_send.at[dx, dy, hr, j], recv_sem=p_recv.at[dx, dz, hr],
-            device_id=(y, lax.rem(x + dx, nx) * CORES + core, to_z), device_id_type=MESH)
+            device_id=(y, gy, to_z), device_id_type=MESH)
         return to_z, copy
 
     for dx, dy in blocks:
@@ -80,14 +80,31 @@
             send_buf[dx, dy, hr] = part.astype(BF16)
             for j in range(per_block):
                 to_z, copy = chunk(dx, dy, hr, j)
-                if dx:
-                    copy.start()
-                else:
-                    pl.when(to_z != z)(copy.start)
+                pl.when(to_z != z)(copy.start)
 
-                    @pl.when(to_z == z)
-                    def _():
-                        own[hr] = part[j * out_rows:(j + 1) * out_rows]
+                @pl.when(to_z == z)
+                def _():
+                    own[dx, hr] = part[j * out_rows:(j + 1) * out_rows]
+
+    def reduced(dx, hr):
+        acc = own[dx, hr]
+        for dz in range(1, nz):
+            pltpu.make_async_remote_copy(
+                src_ref=send_buf.at[0, 0, hr, pl.ds(0, out_rows)], dst_ref=recv.at[dx, dz, hr],
+                send_sem=p_send.at[0, 0, hr, 0], recv_sem=p_recv.at[dx, dz, hr],
+                device_id=partner, device_id_type=MESH).wait_recv()
+            acc = acc + recv[dx, dz, hr].astype(F32)
+        return acc
+
+    back_copies = {}
+    for dx in range(1, nx):
+        for hr in range(CORES):
+            back[0, dx, hr] = reduced(dx, hr).astype(BF16)
+            back_copies[dx, hr] = pltpu.make_async_remote_copy(
+                src_ref=back.at[0, dx, hr], dst_ref=back.at[1, dx, hr],
+                send_sem=b_send.at[dx, hr], recv_sem=b_recv.at[dx, hr],
+                device_id=at(dx, 0, 0), device_id_type=MESH)
+            back_copies[dx, hr].start()
 
     res_in.wait()
     total = jnp.zeros((out_rows, 128), F32)
@@ -96,16 +113,11 @@
         for hr in range(CORES):
             half = core if hr == 0 else 1 - core
             where = pl.ds(pl.multiple_of((from_x * CORES + half) * wc, wc), wc)
-            acc = own[hr] if dx == 0 else None
-            for dz in range(nz):
-                if (dx, dz) == (0, 0):
-                    continue
-                pltpu.make_async_remote_copy(
-                    src_ref=send_buf.at[0, 0, hr, pl.ds(0, out_rows)], dst_ref=recv.at[dx, dz, hr],
-                    send_sem=p_send.at[0, 0, hr, 0], recv_sem=p_recv.at[dx, dz, hr],
-                    device_id=partner, device_id_type=MESH).wait_recv()
-                term = recv[dx, dz, hr].astype(F32)
-                acc = term if acc is None else acc + term
+            if dx:
+                back_copies[dx, hr].wait_recv()
+                acc = back[1, dx, hr].astype(F32)
+            else:
+                acc = reduced(0, hr)
             hidden = (res_v[:, where].astype(F32) + acc).astype(BF16)
             hid_ref[:, where] = hidden
             wide = hidden.astype(F32)
@@ -121,16 +133,13 @@
         sum_copies[-1].start()
 
     w_copy.wait_send()
-    for copy in head_copies.values():
+    for copy in list(head_copies.values()) + list(back_copies.values()):
         copy.wait_send()
     for dx, dy in blocks:
         for hr in range(CORES):
             for j in range(per_block):
                 to_z, copy = chunk(dx, dy, hr, j)
-                if dx:
-                    copy.wait_send()
-                else:
-                    pl.when(to_z != z)(copy.wait_send)
+                pl.when(to_z != z)(copy.wait_send)
     squares = sums[0]
     for dy, copy in enumerate(sum_copies, 1):
         copy.wait()
@@ -162,10 +171,12 @@
             pltpu.VMEM((out_rows, cols), BF16),
             pltpu.VMEM((nx, ny, CORES, in_rows, wc), BF16),
             pltpu.VMEM((nx, nz, CORES, out_rows, wc), BF16),
-            pltpu.VMEM((CORES, out_rows, wc), F32),
+            pltpu.VMEM((nx, CORES, out_rows, wc), F32),
+            pltpu.VMEM((2, nx, CORES, out_rows, wc), BF16),
             pltpu.VMEM((ny, out_rows, 128), F32),
             dma((3,)), dma, dma, dma((nx, ny)), dma((nx, ny)),
             dma((nx, ny, CORES, per_block)), dma((nx, nz, CORES)),
+            dma((nx, CORES)), dma((nx, CORES)),
             dma((ny,)), dma((ny,)),
         ],
         compiler_params=pltpu.CompilerParams(collective_id=0, has_side_effects=True),

time: 38.2 us -> 41.5 us (1.086)
  Pallas kernels: 33.6 us -> 36.9 us
    pallas_call x1, Pallas kernels: 33.6 us -> 36.9 us  [shards(): pl.pallas_call(functools.partial(kernel, ny, ngy, nz), out_shape=[jax.Sha...]
where the time goes in v2:
time: 41.5 us; the launch traced here: 41.2 us
  Pallas kernels  36.9 us (89%)
  local copies, waits for them, and re-layouts  2.34 us (6%)
  other arithmetic  1.3 us (3%)
  between operations  0.65 us (2%)
    pallas_call x1, Pallas kernels, shards(): pl.pallas_call(functools.partial(kernel, ny, ngy, nz), out_shape=[jax.Sha...  36.9 us
    unnamed x4, local copies, waits for them, and re-layouts  2.34 us
    reshape x1, other arithmetic, shards(): norm_gain.astype(F32).reshape(1, -1)  1.3 us

profile of v2, /device:TPU:0, one launch (start us, length us, event | category | flops | bytes accessed | tf_op | source)
XLA Modules:
  0.0 41.2 jit_solution(13928093501791780692)
XLA Ops:
  0.6 1.3 %reshape.11 = f32[4096]{0:T(1024)} convert(bf16[4096]{0:T(1024)(128)(2,1)} %param.7) | non-fusion elementwise | flops 4096 | bytes 24576 | tf_op jit(solution)/shard_map/reshape | solution.py:183
  1.9 36.9 %shard_map.59 = (bf16[48,2048]{1,0:T(8,128)(2,1)}, bf16[48,2048]{1,0:T(8,128)(2,1)}) custom-call(bf16[96,1024]{1,0:T(8,128)(2,1)} %head_ref.1, bf16[1024,512]{1,0:T(8,128)(2,1)} %w_ref.1, bf16[48,2048]{1,0:T(8,128)(2,1)} %res_ref.1, f32[1,4096]{1,0:T(1,128)} %bitcast.1), custom_call_target="tpu_custom_call" | custom-call | tf_op jit(solution)/shard_map/pallas_call | solution.py:162
  38.8 0.0 copy-start
  38.8 1.7 %copy.8 = bf16[48,2048]{1,0:T(8,128)(2,1)} copy(bf16[48,2048]{1,0:T(8,128)(2,1)} %get-tuple-element.4) | data formatting | bytes 393216
  40.5 0.0 copy-done
  40.5 0.7 %copy.9 = bf16[48,2048]{1,0:T(8,128)(2,1)} copy(bf16[48,2048]{1,0:T(8,128)(2,1)S(1)} %copy-done) | data formatting | bytes 393216
Async XLA Ops:
  38.8 1.7 %copy-start = (bf16[48,2048]{1,0:T(8,128)(2,1)S(1)}, bf16[48,2048]{1,0:T(8,128)(2,1)}, u32[]{:S(2)}) copy-start(bf16[48,2048]{1,0:T(8,128)(2,1)} %get-tuple-element.5) | copy-start | bytes 589828

commit v3 on v1

--- a/solution.py
+++ b/solution.py
@@ -136,7 +136,7 @@
         copy.wait()
         squares = squares + sums[dy]
     inverse = lax.rsqrt(squares / (cols * ny) + 1e-05)[:, :1]
-    gain = gain_ref[:, pl.ds(pl.multiple_of(y * cols, cols), cols)]
+    gain = gain_ref[pl.ds(pl.multiple_of(y * cols, cols), cols)].astype(F32).reshape(1, cols)
     nrm_ref[...] = (hid_ref[...].astype(F32) * inverse * gain).astype(BF16)
 
 
@@ -169,7 +169,7 @@
             dma((ny,)), dma((ny,)),
         ],
         compiler_params=pltpu.CompilerParams(collective_id=0, has_side_effects=True),
-    )(head_out, out_weight, residual, norm_gain.astype(F32).reshape(1, -1))
+    )(head_out, out_weight, residual, norm_gain)
 
 
 def solution(mesh):

time: 38.2 us -> 36.8 us (0.963)
  other arithmetic: 1.3 us -> 0 us
    reshape x1 -> x0, other arithmetic: 1.3 us -> none  [shards(): norm_gain.astype(F32).reshape(1, -1)]
where the time goes in v3:
time: 36.8 us; the launch traced here: 36.6 us
  Pallas kernels  33.6 us (91%)
  local copies, waits for them, and re-layouts  2.34 us (6%)
  between operations  0.65 us (2%)
    pallas_call x1, Pallas kernels, shards(): pl.pallas_call(functools.partial(kernel, ny, ngy, nz), out_shape=[jax.Sha...  33.6 us
    unnamed x4, local copies, waits for them, and re-layouts  2.34 us

profile of v3, /device:TPU:0, one launch (start us, length us, event | category | flops | bytes accessed | tf_op | source)
XLA Modules:
  0.0 36.6 jit_solution(13728688314581159124)
XLA Ops:
  0.6 33.6 %shard_map.59 = (bf16[48,2048]{1,0:T(8,128)(2,1)}, bf16[48,2048]{1,0:T(8,128)(2,1)}) custom-call(bf16[96,1024]{1,0:T(8,128)(2,1)} %head_ref.1, bf16[1024,512]{1,0:T(8,128)(2,1)} %w_ref.1, bf16[48,2048]{1,0:T(8,128)(2,1)} %res_ref.1, bf16[4096]{0:T(1024)(128)(2,1)} %gain_ref.1), custom_call_target="tpu_custom_call" | custom-call | tf_op jit(solution)/shard_map/pallas_call | solution.py:153
  34.3 0.0 copy-start
  34.3 1.7 %copy.8 = bf16[48,2048]{1,0:T(8,128)(2,1)} copy(bf16[48,2048]{1,0:T(8,128)(2,1)} %get-tuple-element.4) | data formatting | bytes 393216
  35.9 0.0 copy-done
  35.9 0.7 %copy.9 = bf16[48,2048]{1,0:T(8,128)(2,1)} copy(bf16[48,2048]{1,0:T(8,128)(2,1)S(1)} %copy-done) | data formatting | bytes 393216
Async XLA Ops:
  34.3 1.7 %copy-start = (bf16[48,2048]{1,0:T(8,128)(2,1)S(1)}, bf16[48,2048]{1,0:T(8,128)(2,1)}, u32[]{:S(2)}) copy-start(bf16[48,2048]{1,0:T(8,128)(2,1)} %get-tuple-element.5) | copy-start | bytes 589828

commit v4 on v3

--- a/solution.py
+++ b/solution.py
@@ -46,7 +46,7 @@
     head_in.wait()
     pl.semaphore_wait(barrier, len(offsets) + 1)
 
-    blocks = sorted(((dx, dy) for dx in range(nx) for dy in range(ny)), key=lambda b: ((b[0] > 0) + (b[1] > 0), b))
+    blocks = sorted(((dx, dy) for dx in range(nx) for dy in range(ny)), key=lambda b: ((b[0] > 0) + (b[1] > 0), -b[0], b))
     head_copies = {}
     for dx, dy in blocks[1:]:
         head_copies[dx, dy] = pltpu.make_async_remote_copy(

time: 36.8 us -> 38.3 us (1.041)
  Pallas kernels: 33.6 us -> 35.1 us
    pallas_call x1, Pallas kernels: 33.6 us -> 35.1 us  [shards(): pl.pallas_call(functools.partial(kernel, ny, ngy, nz), out_shape=[jax.Sha...]
where the time goes in v4:
time: 38.3 us; the launch traced here: 38.1 us
  Pallas kernels  35.1 us (92%)
  local copies, waits for them, and re-layouts  2.34 us (6%)
  between operations  0.65 us (2%)
    pallas_call x1, Pallas kernels, shards(): pl.pallas_call(functools.partial(kernel, ny, ngy, nz), out_shape=[jax.Sha...  35.1 us
    unnamed x4, local copies, waits for them, and re-layouts  2.34 us

profile of v4, /device:TPU:0, one launch (start us, length us, event | category | flops | bytes accessed | tf_op | source)
XLA Modules:
  0.0 38.1 jit_solution(7473154453531097976)
XLA Ops:
  0.6 35.1 %shard_map.59 = (bf16[48,2048]{1,0:T(8,128)(2,1)}, bf16[48,2048]{1,0:T(8,128)(2,1)}) custom-call(bf16[96,1024]{1,0:T(8,128)(2,1)} %head_ref.1, bf16[1024,512]{1,0:T(8,128)(2,1)} %w_ref.1, bf16[48,2048]{1,0:T(8,128)(2,1)} %res_ref.1, bf16[4096]{0:T(1024)(128)(2,1)} %gain_ref.1), custom_call_target="tpu_custom_call" | custom-call | tf_op jit(solution)/shard_map/pallas_call | solution.py:153
  35.7 0.0 copy-start
  35.7 1.7 %copy.8 = bf16[48,2048]{1,0:T(8,128)(2,1)} copy(bf16[48,2048]{1,0:T(8,128)(2,1)} %get-tuple-element.4) | data formatting | bytes 393216
  37.4 0.0 copy-done
  37.4 0.7 %copy.9 = bf16[48,2048]{1,0:T(8,128)(2,1)} copy(bf16[48,2048]{1,0:T(8,128)(2,1)S(1)} %copy-done) | data formatting | bytes 393216
Async XLA Ops:
  35.7 1.7 %copy-start = (bf16[48,2048]{1,0:T(8,128)(2,1)S(1)}, bf16[48,2048]{1,0:T(8,128)(2,1)}, u32[]{:S(2)}) copy-start(bf16[48,2048]{1,0:T(8,128)(2,1)} %get-tuple-element.5) | copy-start | bytes 589828
